TPU v7x, 32 devices: a whole 2x2x4 slice. The times are simulated.
32 devices in a mesh: rep: 2 (over y), seq: 4 (over z), tp: 4 (over x, core).
Axes of the slice: x: 2, y: 2, z: 4, core: 2. Of those that a mesh axis runs over, the one named last changes fastest.
Arguments:
- queries: bfloat16 [128, 64, 128], P(('rep', 'seq')), parts along dimension 0, may hold values from -9 to 9
- key_pages: bfloat16 [1024, 8, 64, 128], P(('rep', 'seq'), 'tp'), parts along dimension 0, may hold values from -4 to 4
- value_pages: bfloat16 [1024, 8, 64, 128], P(('rep', 'seq'), 'tp'), parts along dimension 0, may hold values from -6 to 6
- page_owner: int32 [128, 128], P('rep'), parts along dimension 0, may hold values from 0 to 3, as said below
- page_local: int32 [128, 128], P('rep'), parts along dimension 0, may hold values from 0 to 127, as said below
- seq_lengths: int32 [128], P('rep'), parts along dimension 0, may hold values from 1 to 8192, as said below
Outputs:
- attention: bfloat16 [128, 64, 128], P(('rep', 'seq'), 'tp'), parts along dimension 0
There are 2 independent parts, one for each index of `rep`. A program takes and returns all parts, laid end to end along the dimension named above; each array names one. Nothing has to cross between parts.
Inputs may be any that keep to these rules, and one draw needn't show every extreme that they name: The live slots (s * 64 < seq_lengths[b]) name pairs (page_owner, page_local) that are all different; the other slots hold 0. `page_local`: see page_owner. `seq_lengths`: one sequence has exactly 8192 tokens; the live slots of all sequences together number at most half of the 512 pages.
All inputs are finite; a program needn't handle non-finite values.
Results may differ from a plain program's by a relative error of at most 0.008.
Values may be sent and summed in bfloat16 or wider, within the bound.
A program may use at most 64 MiB of HBM per device.

v0:
```python
import math
import jax
import jax.numpy as jnp
from jax import lax
from jax.sharding import PartitionSpec as P

HQ = 64
KVH = 8
score_shift = 8.0


def body(queries, key_pages, value_pages, page_owner, page_local, seq_lengths):
    seq_count = page_owner.shape[0]
    slot_count = page_owner.shape[1]
    pool_pages = key_pages.shape[0]
    kv_local = key_pages.shape[1]
    page_len = key_pages.shape[2]
    head_dim = key_pages.shape[3]
    group_size = HQ // KVH
    heads_local = kv_local * group_size
    seq_rank = lax.axis_index("seq")
    tp_rank = lax.axis_index("tp")
    slot_ids = jnp.arange(slot_count, dtype=jnp.int32)
    slot_fill = jnp.clip(seq_lengths[:, None] - slot_ids[None, :] * page_len, 0, page_len)
    owned = (slot_fill > 0) & (page_owner == seq_rank)
    pool_range = jnp.arange(pool_pages, dtype=jnp.int32)
    matches = ((page_local[:, :, None] == pool_range[None, None, :]) & owned[:, :, None]).astype(
        jnp.bfloat16
    )
    fill_weight = slot_fill.astype(jnp.bfloat16)
    fill_table = jnp.einsum("bsp,bs->bp", matches, fill_weight, preferred_element_type=jnp.float32)
    hit_table = jnp.sum(matches.astype(jnp.float32), axis=1)
    seq_weight = jnp.arange(seq_count, dtype=jnp.float32)
    page_seq = jnp.dot(seq_weight, hit_table, precision=lax.Precision.HIGHEST).astype(jnp.int32)
    page_fill = jnp.sum(fill_table, axis=0).astype(jnp.int32)
    local_heads = lax.dynamic_slice_in_dim(queries, tp_rank * heads_local, heads_local, 1)
    head_queries = lax.all_gather(local_heads, "seq", axis=0, tiled=True)
    query_flat = head_queries.reshape(seq_count, heads_local * head_dim)
    score_scale = 1.0 / math.sqrt(head_dim)
    seq_range = jnp.arange(seq_count, dtype=jnp.int32)
    count = page_seq.shape[0]
    selector = page_seq[:, None] == seq_range[None, :]
    picked = jnp.dot(
        selector.astype(jnp.bfloat16), query_flat, preferred_element_type=jnp.float32
    ).astype(jnp.bfloat16)
    picked = picked.reshape(count, kv_local, group_size, head_dim)
    scores = (
        jnp.einsum("pkgd,pktd->pkgt", picked, key_pages, preferred_element_type=jnp.float32)
        * score_scale
    )
    live_mask = jnp.arange(page_len, dtype=jnp.int32)[None, :] < page_fill[:, None]
    weight = jnp.where(live_mask[:, None, None, :], jnp.exp(scores - score_shift), 0.0)
    page_total = jnp.sum(weight, axis=-1)
    page_sum = jnp.einsum(
        "pkgt,pktd->pkgd",
        weight.astype(jnp.bfloat16),
        value_pages,
        preferred_element_type=jnp.float32,
    )
    spread = selector.astype(jnp.float32).T
    numerator = jnp.dot(
        spread, page_sum.reshape(count, heads_local * head_dim), precision=lax.Precision.HIGHEST
    )
    denominator = jnp.dot(
        spread, page_total.reshape(count, heads_local), precision=lax.Precision.HIGHEST
    )
    numerator, denominator = (numerator, denominator)
    own_rows = seq_count // lax.axis_size("seq")
    summed_num, summed_den = lax.psum((numerator, denominator), "seq")
    summed_num = lax.dynamic_slice_in_dim(summed_num, seq_rank * own_rows, own_rows, 0)
    summed_den = lax.dynamic_slice_in_dim(summed_den, seq_rank * own_rows, own_rows, 0)
    result = summed_num.reshape(own_rows, heads_local, head_dim) / summed_den[..., None]
    return result.astype(jnp.bfloat16)


def solution(mesh):
    placed = (
        P(("rep", "seq"), None, None),
        P(("rep", "seq"), "tp", None, None),
        P(("rep", "seq"), "tp", None, None),
        P("rep", None),
        P("rep", None),
        P("rep"),
    )
    return jax.shard_map(
        body, mesh=mesh, in_specs=placed, out_specs=P(("rep", "seq"), "tp", None), check_vma=False
    )
```

profile of v0, /device:TPU:0, one launch (start us, length us, event | category | flops | bytes accessed | tf_op | source)
XLA Modules:
  0.0 89.1 jit_solution(877653192962036179)
XLA Ops:
  6.5 0.0 copy-start
  6.5 0.0 all-reduce.2.cloned.1.call-start
  6.5 0.8 fusion.35
  7.3 0.8 fusion.34
  8.2 4.5 %convert_reduce_fusion = f32[64,128]{1,0:T(8,128)S(1)} fusion(s32[64,128]{1,0:T(8,128)} %param.10, pred[64,128]{1,0:T(8,128)(4,1)S(1)} %fusion.34), kind=kLoop, calls=%fused_computation | loop fusion | flops 5234688 | bytes 73728 | tf_op jit(solution)/shard_map/reduce_sum | solution.py:32
  12.7 3.1 %fusion.14 = s32[128]{0:T(128)S(1)} fusion(s32[64,128]{1,0:T(8,128)} %param.10, pred[64,128]{1,0:T(8,128)(4,1)S(1)} %fusion.34, bf16[64,128,1]{1,0,2:T(8,128)(2,1)S(1)} %fusion.35), kind=kOutput, calls=%fused_computation.16 | convolution fusion | flops 4194432 | bytes 57856 | tf_op jit(solution)/shard_map/bsp,bs->bp/dot_general | solution.py:31
  15.8 0.1 iota_compare_fusion.1
  15.9 0.1 fusion.10
  16.0 0.0 copy-done
  16.0 0.0 copy-start.1
  16.1 15.8 %all_gather.3 = bf16[64,16,128]{2,1,0:T(8,128)(2,1)S(1)} all-gather(bf16[16,16,128]{2,1,0:T(8,128)(2,1)S(1)} %constant_dynamic-slice_fusion.1), channel_id=1, replica_groups=mesh['rep'=2,'seq'=4,'tp'=4] {'seq'}, dimensions={0}, use_global_device_ids=true | all-gather | bytes 327680 | tf_op jit(solution)/shard_map/all_gather | solution.py:37
  31.9 0.3 fusion.9
  32.2 0.1 copy.11
  32.3 4.6 %fusion.38 = (f32[128,2,8]{2,1,0:T(2,128)S(1)}, bf16[128,2,8,64]{3,2,1,0:T(8,128)(2,1)S(1)}) fusion(bf16[128,2,8,128]{3,2,1,0:T(8,128)(2,1)S(1)} %bitcast.38, bf16[128,2,64,128]{3,2,1,0:T(8,128)(2,1)} %param.7, pred[128,64]{1,0:T(8,128)(4,1)S(1)} %iota_compare_fusion.1), kind=kOutput, calls=%fused_computation.45 | convolution fusion | flops 34207744 | bytes 4997120 | tf_op jit(solution)/shard_map/pkgd,pktd->pkgt/dot_general | solution.py:48
  37.0 0.0 copy-done.1
  37.0 1.2 %fusion.20 = f32[128,2,8,128]{3,2,1,0:T(8,128)S(1)} fusion(bf16[128,2,64,128]{3,2,1,0:T(8,128)(2,1)S(1)} %copy-done.1, bf16[128,2,8,64]{3,2,1,0:T(8,128)(2,1)S(1)} %get-tuple-element.6), kind=kOutput, calls=%fused_computation.20 | convolution fusion | flops 33554432 | bytes 5505024 | tf_op jit(solution)/shard_map/pkgt,pktd->pkgd/dot_general | solution.py:54
  38.2 1.7 %fusion.17 = f32[64,2048]{1,0:T(8,128)} fusion(f32[16,8,16,128]{3,2,1,0:T(8,128)S(1)} %bitcast.37, s32[128]{0:T(128)S(1)} %fusion.10), kind=kOutput, calls=%fused_computation.17 | convolution fusion | flops 201334784 | bytes 1573376 | tf_op jit(solution)/shard_map/dot_general | solution.py:61
  39.8 0.0 all-reduce.2.cloned.1.call-update
  39.8 0.1 copy.8
  39.9 0.3 fusion.26
  40.2 20.0 %psum.15 = f32[64,16]{1,0:T(8,128)S(1)} all-reduce(f32[64,16]{1,0:T(8,128)S(1)} %fusion.26), channel_id=1, replica_groups=mesh['rep'=2,'seq'=4,'tp'=4] {'seq'}, use_global_device_ids=true, to_apply=%region_3.4 | all-reduce | flops 1024 | bytes 8192 | tf_op jit(solution)/shard_map/psum | solution.py:69
  60.2 20.3 %all-reduce.2.cloned.1.call-done = f32[64,2048]{1,0:T(8,128)} async-done(((f32[64,2048]{1,0:T(8,128)}), f32[64,2048]{1,0:T(8,128)}) %all-reduce.2.cloned.1.call-update) | async-done | bytes 524304 | tf_op jit(solution)/shard_map/psum | solution.py:69
  80.6 0.9 %dynamic-slice_bitcast_fusion = f32[2,8,16,128]{3,1,2,0:T(8,128)S(1)} fusion(f32[64,2048]{1,0:T(8,128)} %all-reduce.2.cloned.1.call-done, s32[]{:T(128)S(6)} %select_n.13), kind=kLoop, calls=%fused_computation.26 | loop fusion | bytes 262148
  81.5 0.7 fusion.24
  (4 shorter events, 0.1 us)
Async XLA Ops:
  6.5 9.5 %copy-start = (bf16[16,64,128]{2,1,0:T(8,128)(2,1)S(1)}, bf16[16,64,128]{2,1,0:T(8,128)(2,1)}, u32[]{:S(2)}) copy-start(bf16[16,64,128]{2,1,0:T(8,128)(2,1)} %param.6) | copy-start | bytes 786436
  6.5 74.0 %all-reduce.2.cloned.1.call-start = ((), (), s32[]{:S(2)}) async-start(), calls=%async_computation | async-start | bytes 1048576 | tf_op jit(solution)/shard_map/psum | solution.py:69
  16.0 20.9 %copy-start.1 = (bf16[128,2,64,128]{3,2,1,0:T(8,128)(2,1)S(1)}, bf16[128,2,64,128]{3,2,1,0:T(8,128)(2,1)}, u32[]{:S(2)}) copy-start(bf16[128,2,64,128]{3,2,1,0:T(8,128)(2,1)} %param.8) | copy-start | bytes 12582916
Sparse Core Ops, SparseCore 0:
  40.0 40.5 all-reduce.1
where the time goes:
time: 89.6 us; the launch traced here: 89.1 us
  blocking collectives  35.8 us (40%)
  waiting for transfers between devices  20.3 us (23%)
  between operations  13.5 us (15%)
  matrix products  11.4 us (13%)
  other arithmetic  6.96 us (8%)
  local copies, waits for them, and re-layouts  1.15 us (1%)
    psum x1, waiting for transfers between devices, body(): summed_num, summed_den = lax.psum((numerator, denominator), 'seq')  20.3 us
    psum x1, blocking collectives, body(): summed_num, summed_den = lax.psum((numerator, denominator), 'seq')  20 us
    all_gather x1, blocking collectives, body(): head_queries = lax.all_gather(local_heads, 'seq', axis=0, tiled=True)  15.8 us
    dot_general x1, matrix products, body(): jnp.einsum('pkgd,pktd->pkgt', picked, key_pages, preferred_element_type=j...  4.63 us
    reduce_sum x1, other arithmetic, body(): hit_table = jnp.sum(matches.astype(jnp.float32), axis=1)  4.51 us
    dot_general x1, matrix products, body(): jnp.einsum('bsp,bs->bp', matches, fill_weight, preferred_element_type=jnp...  3.1 us
  transfers between devices with their start and end apart: 1, of which 1 were waited for; matrix products, arithmetic and copies ran while one was open for 0% of the time, Pallas kernels for 0%

commit v1 on v0

--- a/solution.py
+++ b/solution.py
@@ -3,6 +3,7 @@
 import jax.numpy as jnp
 from jax import lax
 from jax.sharding import PartitionSpec as P
+from jax.lax import axis_index, axis_size, ppermute
 
 HQ = 64
 KVH = 8
@@ -34,7 +35,17 @@
     page_seq = jnp.dot(seq_weight, hit_table, precision=lax.Precision.HIGHEST).astype(jnp.int32)
     page_fill = jnp.sum(fill_table, axis=0).astype(jnp.int32)
     local_heads = lax.dynamic_slice_in_dim(queries, tp_rank * heads_local, heads_local, 1)
-    head_queries = lax.all_gather(local_heads, "seq", axis=0, tiled=True)
+    dev_count = axis_size("seq")
+    parts_out = sorted(((nth, (nth + 1) % dev_count) for nth in range(dev_count)))
+    taken_in = local_heads
+    line_up = [taken_in]
+    for h in range(1, dev_count):
+        taken_in = ppermute(taken_in, axis_name="seq", perm=parts_out)
+        line_up.insert(0, taken_in)
+    shaped = jnp.concatenate(line_up, axis=0)
+    b_next = axis_index("seq")
+    outer = b_next + 1
+    head_queries = jnp.roll(shaped, outer * local_heads.shape[0], axis=0)
     query_flat = head_queries.reshape(seq_count, heads_local * head_dim)
     score_scale = 1.0 / math.sqrt(head_dim)
     seq_range = jnp.arange(seq_count, dtype=jnp.int32)

time: 89.6 us -> 88.4 us (0.987)
  blocking collectives: 35.8 us -> 16.1 us
  waiting for transfers between devices: 20.3 us -> 31.1 us
  starting transfers between devices: 0.01 us -> 4.69 us
  local copies, waits for them, and re-layouts: 1.15 us -> 4.16 us
    all_gather x1 -> x0, blocking collectives: 15.8 us -> none  [body(): head_queries = lax.all_gather(local_heads, 'seq', axis=0, tiled=True)]
    ppermute x0 -> x3, waiting for transfers between devices: none -> 10.3 us  [body(): taken_in = ppermute(taken_in, axis_name='seq', perm=parts_out)]
    ppermute x0 -> x3, starting transfers between devices: none -> 4.68 us  [body(): taken_in = ppermute(taken_in, axis_name='seq', perm=parts_out)]
    psum x1, blocking collectives: 20 us -> 16.1 us  [body(): summed_num, summed_den = lax.psum((numerator, denominator), 'seq')]
    unnamed x7 -> x12, local copies, waits for them, and re-layouts: 1.06 us -> 2.15 us
    concatenate x0 -> x1, local copies, waits for them, and re-layouts: none -> 1.07 us  [body(): head_queries = jnp.roll(shaped, outer * local_heads.shape[0], axis=0)]
  transfers between devices with their start and end apart: 1 -> 4, of which waited for: 1 -> 3; matrix products, arithmetic and copies ran while one was open for 0% -> 11% of each run, Pallas kernels for 0% -> 0%
where the time goes in v1:
time: 88.4 us; the launch traced here: 87.8 us
  waiting for transfers between devices  31.1 us (35%)
  blocking collectives  16.1 us (18%)
  between operations  13.6 us (15%)
  matrix products  11.4 us (13%)
  other arithmetic  6.9 us (8%)
  starting transfers between devices  4.69 us (5%)
  local copies, waits for them, and re-layouts  4.16 us (5%)
    psum x1, waiting for transfers between devices, body(): summed_num, summed_den = lax.psum((numerator, denominator), 'seq')  20.7 us
    psum x1, blocking collectives, body(): summed_num, summed_den = lax.psum((numerator, denominator), 'seq')  16.1 us
    ppermute x3, waiting for transfers between devices, body(): taken_in = ppermute(taken_in, axis_name='seq', perm=parts_out)  10.3 us
    ppermute x3, starting transfers between devices, body(): taken_in = ppermute(taken_in, axis_name='seq', perm=parts_out)  4.68 us
    dot_general x1, matrix products, body(): jnp.einsum('pkgd,pktd->pkgt', picked, key_pages, preferred_element_type=j...  4.63 us
    reduce_sum x1, other arithmetic, body(): hit_table = jnp.sum(matches.astype(jnp.float32), axis=1)  4.51 us
    dot_general x1, matrix products, body(): jnp.einsum('bsp,bs->bp', matches, fill_weight, preferred_element_type=jnp...  3.1 us
    unnamed x12, local copies, waits for them, and re-layouts  2.15 us
  transfers between devices with their start and end apart: 4, of which 3 were waited for; matrix products, arithmetic and copies ran while one was open for 11% of the time, Pallas kernels for 0%

profile of v1, /device:TPU:0, one launch (start us, length us, event | category | flops | bytes accessed | tf_op | source)
XLA Modules:
  0.0 87.8 jit_solution(15224476766246300852)
XLA Ops:
  6.5 0.8 constant_dynamic-slice_fusion.2
  7.4 3.1 %collective-permute-start = (bf16[16,16,128]{2,1,0:T(8,128)(2,1)S(1)}, bf16[16,16,128]{2,1,0:T(8,128)(2,1)S(1)}, u32[]{:S(2)}, u32[]{:S(2)}) collective-permute-start(bf16[16,16,128]{2,1,0:T(8,128)(2,1)S(1)} %constant_dynamic-slice_fusion.2), channel_id=1, source_target_pairs={{0,4},{4,8},{8,12},{12,0},{1,5},{5,9},{9,13},{13,1},{2,6},{6,10},{... | collective-permute-start | bytes 196616 | tf_op jit(solution)/shard_map/ppermute | solution.py:43
  10.4 0.7 fusion.35
  11.2 0.8 fusion.34
  12.0 3.1 %fusion.14 = s32[128]{0:T(128)S(1)} fusion(s32[64,128]{1,0:T(8,128)} %param.10, pred[64,128]{1,0:T(8,128)(4,1)S(1)} %fusion.34, bf16[64,128,1]{1,0,2:T(8,128)(2,1)S(1)} %fusion.35), kind=kOutput, calls=%fused_computation.16 | convolution fusion | flops 4194432 | bytes 57856 | tf_op jit(solution)/shard_map/bsp,bs->bp/dot_general | solution.py:32
  15.1 4.5 %convert_reduce_fusion = f32[64,128]{1,0:T(8,128)S(1)} fusion(s32[64,128]{1,0:T(8,128)} %param.10, pred[64,128]{1,0:T(8,128)(4,1)S(1)} %fusion.34), kind=kLoop, calls=%fused_computation | loop fusion | flops 5234688 | bytes 73728 | tf_op jit(solution)/shard_map/reduce_sum | solution.py:33
  19.6 1.6 %collective-permute-start.1 = (bf16[16,16,128]{2,1,0:T(8,128)(2,1)S(1)}, bf16[16,16,128]{2,1,0:T(8,128)(2,1)S(1)}, u32[]{:S(2)}, u32[]{:S(2)}) collective-permute-start(bf16[16,16,128]{2,1,0:T(8,128)(2,1)S(1)} %collective-permute-done), channel_id=1, source_target_pairs={{0,4},{4,8},{8,12},{12,0},{1,5},{5,9},{9,13},{13,1},{2,6},{6,10},{... | collective-permute-start | bytes 196616 | tf_op jit(solution)/shard_map/ppermute | solution.py:43
  21.3 0.1 fusion.10
  21.4 4.3 %collective-permute-done.1 = bf16[16,16,128]{2,1,0:T(8,128)(2,1)S(1)} collective-permute-done((bf16[16,16,128]{2,1,0:T(8,128)(2,1)S(1)}, bf16[16,16,128]{2,1,0:T(8,128)(2,1)S(1)}, u32[]{:S(2)}, u32[]{:S(2)}) %collective-permute-start.1) | collective-permute-done | bytes 65568 | tf_op jit(solution)/shard_map/ppermute | solution.py:43
  25.8 0.1 iota_compare_fusion.1
  25.9 6.0 %collective-permute-done.2 = bf16[16,16,128]{2,1,0:T(8,128)(2,1)S(1)} collective-permute-done((bf16[16,16,128]{2,1,0:T(8,128)(2,1)S(1)}, bf16[16,16,128]{2,1,0:T(8,128)(2,1)S(1)}, u32[]{:S(2)}, u32[]{:S(2)}) %collective-permute-start.2) | collective-permute-done | bytes 65568 | tf_op jit(solution)/shard_map/ppermute | solution.py:43
  31.9 1.0 %constant_dynamic-update-slice_fusion.4 = bf16[128,16,128]{2,1,0:T(8,128)(2,1)S(1)} fusion(bf16[128,16,128]{2,1,0:T(8,128)(2,1)S(1)} %constant_dynamic-update-slice_fusion.5, bf16[16,64,128]{2,1,0:T(8,128)(2,1)} %param.6, s32[]{:T(128)S(6)} %select_n.24), kind=kLoop, calls=%fused_computation.43 | loop fusion | bytes 131076
  33.0 1.1 %constant_dynamic-update-slice_fusion = bf16[128,16,128]{2,1,0:T(8,128)(2,1)S(1)} fusion(bf16[128,16,128]{2,1,0:T(8,128)(2,1)S(1)} %constant_dynamic-update-slice_fusion.1, bf16[16,64,128]{2,1,0:T(8,128)(2,1)} %param.6, s32[]{:T(128)S(6)} %select_n.24), kind=kLoop, calls=%fused_computation.39 | loop fusion | bytes 131076 | tf_op jit(solution)/shard_map/jit(_roll_dynamic)/concatenate | solution.py:48
  34.1 0.3 fusion.9
  34.4 0.1 copy.11
  34.5 4.6 %fusion.38 = (f32[128,2,8]{2,1,0:T(2,128)S(1)}, bf16[128,2,8,64]{3,2,1,0:T(8,128)(2,1)S(1)}) fusion(bf16[128,2,8,128]{3,2,1,0:T(8,128)(2,1)S(1)} %bitcast.38, bf16[128,2,64,128]{3,2,1,0:T(8,128)(2,1)} %param.7, pred[128,64]{1,0:T(8,128)(4,1)S(1)} %iota_compare_fusion.1), kind=kOutput, calls=%fused_computation.54 | convolution fusion | flops 34207744 | bytes 4997120 | tf_op jit(solution)/shard_map/pkgd,pktd->pkgt/dot_general | solution.py:59
  39.2 1.2 %fusion.20 = f32[128,2,8,128]{3,2,1,0:T(8,128)S(1)} fusion(bf16[128,2,64,128]{3,2,1,0:T(8,128)(2,1)S(1)} %copy-done, bf16[128,2,8,64]{3,2,1,0:T(8,128)(2,1)S(1)} %get-tuple-element.6), kind=kOutput, calls=%fused_computation.20 | convolution fusion | flops 33554432 | bytes 5505024 | tf_op jit(solution)/shard_map/pkgt,pktd->pkgd/dot_general | solution.py:65
  40.4 1.7 %fusion.17 = f32[64,2048]{1,0:T(8,128)} fusion(f32[16,8,16,128]{3,2,1,0:T(8,128)S(1)} %bitcast.37, s32[128]{0:T(128)S(1)} %fusion.10), kind=kOutput, calls=%fused_computation.17 | convolution fusion | flops 201334784 | bytes 1573376 | tf_op jit(solution)/shard_map/dot_general | solution.py:72
  42.0 0.1 copy.8
  42.1 0.3 fusion.26
  42.4 16.1 %psum.15 = f32[64,16]{1,0:T(8,128)S(1)} all-reduce(f32[64,16]{1,0:T(8,128)S(1)} %fusion.26), channel_id=1, replica_groups=mesh['rep'=2,'seq'=4,'tp'=4] {'seq'}, use_global_device_ids=true, to_apply=%region_3.4 | all-reduce | flops 1024 | bytes 8192 | tf_op jit(solution)/shard_map/psum | solution.py:80
  58.6 20.7 %all-reduce.2.cloned.1.call-done = f32[64,2048]{1,0:T(8,128)} async-done(((f32[64,2048]{1,0:T(8,128)}), f32[64,2048]{1,0:T(8,128)}) %all-reduce.2.cloned.1.call-update) | async-done | bytes 524304 | tf_op jit(solution)/shard_map/psum | solution.py:80
  79.3 0.9 %dynamic-slice_bitcast_fusion = f32[2,8,16,128]{3,1,2,0:T(8,128)S(1)} fusion(f32[64,2048]{1,0:T(8,128)} %all-reduce.2.cloned.1.call-done, s32[]{:T(128)S(6)} %select_n.28), kind=kLoop, calls=%fused_computation.26 | loop fusion | bytes 262148
  80.2 0.7 fusion.24
  (16 shorter events, 0.2 us)
Async XLA Ops:
  6.5 72.8 %all-reduce.2.cloned.1.call-start = ((), (), s32[]{:S(2)}) async-start(), calls=%async_computation | async-start | bytes 1048576 | tf_op jit(solution)/shard_map/psum | solution.py:80
  7.4 12.3 %collective-permute-start = (bf16[16,16,128]{2,1,0:T(8,128)(2,1)S(1)}, bf16[16,16,128]{2,1,0:T(8,128)(2,1)S(1)}, u32[]{:S(2)}, u32[]{:S(2)}) collective-permute-start(bf16[16,16,128]{2,1,0:T(8,128)(2,1)S(1)} %constant_dynamic-slice_fusion.2), channel_id=1, source_target_pairs={{0,4},{4,8},{8,12},{12,0},{1,5},{5,9},{9,13},{13,1},{2,6},{6,10},{... | collective-permute-start | bytes 196616 | tf_op jit(solution)/shard_map/ppermute | solution.py:43
  19.6 6.1 %collective-permute-start.1 = (bf16[16,16,128]{2,1,0:T(8,128)(2,1)S(1)}, bf16[16,16,128]{2,1,0:T(8,128)(2,1)S(1)}, u32[]{:S(2)}, u32[]{:S(2)}) collective-permute-start(bf16[16,16,128]{2,1,0:T(8,128)(2,1)S(1)} %collective-permute-done), channel_id=1, source_target_pairs={{0,4},{4,8},{8,12},{12,0},{1,5},{5,9},{9,13},{13,1},{2,6},{6,10},{... | collective-permute-start | bytes 196616 | tf_op jit(solution)/shard_map/ppermute | solution.py:43
  25.8 6.1 %collective-permute-start.2 = (bf16[16,16,128]{2,1,0:T(8,128)(2,1)S(1)}, bf16[16,16,128]{2,1,0:T(8,128)(2,1)S(1)}, u32[]{:S(2)}, u32[]{:S(2)}) collective-permute-start(bf16[16,16,128]{2,1,0:T(8,128)(2,1)S(1)} %collective-permute-done.1), channel_id=1, source_target_pairs={{0,4},{4,8},{8,12},{12,0},{1,5},{5,9},{9,13},{13,1},{2,6},{6,10},{... | collective-permute-start | bytes 196616 | tf_op jit(solution)/shard_map/ppermute | solution.py:43
  31.9 7.3 %copy-start = (bf16[128,2,64,128]{3,2,1,0:T(8,128)(2,1)S(1)}, bf16[128,2,64,128]{3,2,1,0:T(8,128)(2,1)}, u32[]{:S(2)}) copy-start(bf16[128,2,64,128]{3,2,1,0:T(8,128)(2,1)} %param.8) | copy-start | bytes 12582916
Sparse Core Ops, SparseCore 0:
  42.2 37.0 all-reduce.1
